TPU v7x, 128 devices: a whole 4x4x4 slice. The times are simulated.
128 devices in a mesh: dp: 16 (over y_hi, x, core), mp: 8 (over z, y_lo).
Axes of the slice: x: 4, y: 4 (y_hi: 2, y_lo: 2; y = y_hi * 2 + y_lo), z: 4, core: 2. Of those that a mesh axis runs over, the one named last changes fastest.
Arguments:
- hidden_states: bfloat16 [65536, 4096], P('dp', 'mp'), may hold values from -1 to 1
- factor_values: bfloat16 [65536, 128], P('dp', 'mp'), may hold values from 0.029907227 to 0.13964844
- class_ids: int32 [65536, 128], P('dp', 'mp'), may hold values from 0 to 128255, as said below
- centers: int32 [3], replicated, may hold values from 0 to 65535
Outputs:
- min_distance: float32 [65536], P(('dp', 'mp'))
- weight_means: float32 [3], replicated
Inputs may be any that keep to these rules, and one draw needn't show every extreme that they name: `centers`: each value is a sample index. `class_ids`: entries k * 16 to (k + 1) * 16 - 1 of a row hold distinct classes of the k-th of 8 equal ranges of the vocabulary.
All inputs are finite; a program needn't handle non-finite values.
Results may differ from a plain program's by a relative error of at most 0.00095.
Values may be sent and summed in bfloat16 or wider, within the bound.
A program may use at most 64 MiB of HBM per device.

v0:
```python
import functools

import jax
import jax.numpy as jnp
from jax import lax
from jax.experimental import pallas as pl
from jax.experimental.pallas import tpu as pltpu
from jax.sharding import PartitionSpec as P

MESH = pl.DeviceIdType.MESH
STEPS = 3
LANES = 128
TALL = 16
CHUNKS = 8
NT = (((1,), (1,)), ((), ()))


def partner(p, k, n):
    if n & (n - 1):
        return lax.rem(p + k, n)
    bit = 1
    q = p
    while bit <= k:
        if k & bit:
            q = q + bit - 2 * bit * lax.rem(lax.div(p, bit), 2)
        bit *= 2
    return q


def drain(ref, sem):
    pltpu.make_async_copy(ref, ref, sem).wait()


def finish(low_ref, mean_ref, dist_ref, means_ref):
    dist_ref[...] = low_ref[...]
    means_ref[...] = mean_ref[0:STEPS]


def kernel(
    DP, MP,
    c_hbm, h_hbm, v_hbm, i_hbm,
    dist_ref, mean_ref,
    c_ref, h, v, ids, ch_buf, ch_slots, sq, sq_slots, norm_buf, norm_slots, part, part_slots,
    row_buf, row_slots,
    z_sem, h_sem, i_sem, v_sem, a_send, a_recv, s_send, s_recv, n_send, n_recv, b_send, b_recv,
    d_send, d_recv,
):
    groups, tall, width = h.shape
    rows = groups * tall
    tiles, depth, _ = ids.shape
    blk = rows // MP
    my_dp = lax.axis_index("dp")
    my_mp = lax.axis_index("mp")
    me = my_dp * MP + my_mp
    f32 = jnp.float32
    dp_peers = [partner(my_dp, k, DP) for k in range(DP)]
    mp_peers = [partner(my_mp, k, MP) for k in range(MP)]

    pltpu.make_async_copy(c_hbm, c_ref, z_sem).start()
    step = max(groups // CHUNKS, 1)
    for j in range(0, groups, step):
        at = pl.ds(j, step)
        pltpu.make_async_copy(h_hbm.at[at], h.at[at], h_sem).start()
    for j in range(tiles):
        at = pl.ds(j * LANES, LANES)
        pltpu.make_async_copy(i_hbm.at[:, at], ids.at[j], i_sem).start()
        pltpu.make_async_copy(v_hbm.at[:, at], v.at[j], v_sem).start()

    barrier = pltpu.get_barrier_semaphore()
    for d in range(1, DP):
        pl.semaphore_signal(
            barrier, inc=1, device_id=(lax.rem(my_dp + d, DP), my_mp), device_id_type=MESH
        )
    for d in range(1, MP):
        pl.semaphore_signal(
            barrier, inc=1, device_id=(my_dp, lax.rem(my_mp + d, MP)), device_id_type=MESH
        )
    pltpu.make_async_copy(c_hbm, c_ref, z_sem).wait()
    drain(ids, i_sem)
    drain(v, v_sem)

    lane = lax.broadcasted_iota(jnp.int32, (4 * depth, LANES), 1)
    row16 = lax.broadcasted_iota(jnp.int32, (tall, 1), 0)
    first = my_dp * rows
    offs = [lax.rem(c_ref[t], rows) for t in range(STEPS)]
    meta = jnp.zeros((4 * depth, LANES), f32)
    for t in range(STEPS):
        g = lax.div(offs[t], LANES)
        k = ids[g]
        digits = [(k >> 12).astype(f32), ((k >> 6) & 63).astype(f32), (k & 63).astype(f32)]
        both = jnp.concatenate(digits + [v[g].astype(f32)], axis=0)
        hit = lane + (first + g * LANES) == c_ref[t]
        col = jnp.sum(jnp.where(hit, both, 0.0), axis=1, keepdims=True)
        meta = jnp.where(lane == t, col, meta)
    wide = jnp.concatenate([meta, jnp.zeros((LANES - 4 * depth, LANES), f32)], axis=0).T
    drain(h, h_sem)
    picks = []
    for t in range(STEPS):
        g = lax.div(offs[t], tall)
        hit = row16 + (first + g * tall) == c_ref[t]
        picks.append(jnp.sum(jnp.where(hit, h[g].astype(f32), 0.0), axis=0, keepdims=True))
    tail = [wide[t:t + 1] for t in range(STEPS)] + [jnp.zeros((1, width - STEPS * LANES), f32)]
    picks.append(jnp.concatenate(tail, axis=1))
    ch_buf[...] = jnp.concatenate(picks, axis=0).astype(jnp.bfloat16)

    pl.semaphore_wait(barrier, DP - 1 + MP - 1)
    for k in reversed(range(1, DP)):
        pltpu.make_async_remote_copy(
            src_ref=ch_buf, dst_ref=ch_slots.at[k - 1], send_sem=a_send, recv_sem=a_recv,
            device_id=(dp_peers[k], my_mp), device_id_type=MESH,
        ).start()

    ones = jnp.ones((8, LANES), jnp.bfloat16)
    for b in range(MP):
        y = jnp.zeros((blk // tall, tall, LANES), f32)
        for j in range(width // LANES):
            x = h[b * blk // tall:(b + 1) * blk // tall, :, j * LANES:(j + 1) * LANES].astype(f32)
            y = y + x * x
        y = y.reshape(blk, LANES)
        hi = y.astype(jnp.bfloat16)
        lo = (y - hi.astype(f32)).astype(jnp.bfloat16)
        norm = lax.dot_general(ones, hi, NT, preferred_element_type=f32)
        norm = norm + lax.dot_general(ones, lo, NT, preferred_element_type=f32)
        sq[b, 0:1] = norm[0:1]
        for j in range(blk // LANES):
            a = v[b * blk // LANES + j].astype(f32)
            sq[b, 1:2, j * LANES:(j + 1) * LANES] = jnp.sum(a * a, axis=0, keepdims=True)
    for k in reversed(range(1, MP)):
        pltpu.make_async_remote_copy(
            src_ref=sq.at[mp_peers[k]], dst_ref=sq_slots.at[k - 1], send_sem=s_send, recv_sem=s_recv,
            device_id=(my_dp, mp_peers[k]), device_id_type=MESH,
        ).start()

    drain(ch_slots, a_recv)
    ch4 = ch_buf[...].astype(f32)
    for d in range(DP - 1):
        ch4 = ch4 + ch_slots[d].astype(f32)
    ch = jnp.concatenate([ch4, jnp.zeros_like(ch4)], axis=0).astype(jnp.bfloat16)
    cm = jnp.concatenate(
        [ch4[3:4, t * LANES:(t + 1) * LANES] for t in range(STEPS)]
        + [jnp.zeros((LANES - STEPS, LANES), f32)],
        axis=0,
    )
    nh = jnp.sum(ch4 * ch4, axis=1, keepdims=True)
    lane8 = lax.broadcasted_iota(jnp.int32, (8, LANES), 1)
    cm8 = jnp.where(lane8 >= 3 * depth, cm[0:8], 0.0)
    na = jnp.sum(cm8 * cm8, axis=1, keepdims=True)
    lane1 = lax.broadcasted_iota(jnp.int32, (1, LANES), 1)
    norms = jnp.zeros((1, LANES), f32)
    for t in range(STEPS):
        norms = jnp.where(lane1 == t, nh[t:t + 1], norms)
        norms = jnp.where(lane1 == STEPS + t, na[t:t + 1], norms)
    norm_buf[...] = norms
    for k in reversed(range(1, MP)):
        pltpu.make_async_remote_copy(
            src_ref=norm_buf, dst_ref=norm_slots.at[k - 1], send_sem=n_send, recv_sem=n_recv,
            device_id=(my_dp, mp_peers[k]), device_id_type=MESH,
        ).start()
    cols = cm.T
    id_cols, v_cols = [], []
    for t in range(STEPS):
        col = jnp.broadcast_to(cols[0:4 * depth, t:t + 1], (4 * depth, LANES))
        code = col[0:depth] * 4096.0 + col[depth:2 * depth] * 64.0 + col[2 * depth:3 * depth]
        id_cols.append(code.astype(jnp.int32))
        v_cols.append(col[3 * depth:])

    for k in reversed(range(MP)):
        b = mp_peers[k]
        hb = h[pl.ds(b * (blk // tall), blk // tall)].reshape(blk, width)
        hh = lax.dot_general(ch, hb, NT, preferred_element_type=f32)
        part[b, 0:STEPS] = hh[0:STEPS]
        for j in range(blk // LANES):
            bid = ids[b * (blk // LANES) + j]
            bv = v[b * (blk // LANES) + j].astype(f32)
            for t in range(STEPS):
                w = jnp.zeros((depth, LANES), f32)
                for l in range(depth):
                    w = jnp.where(bid == id_cols[t][l:l + 1], v_cols[t][l:l + 1], w)
                part[b, STEPS + t:STEPS + t + 1, j * LANES:(j + 1) * LANES] = jnp.sum(
                    bv * w, axis=0, keepdims=True
                )
        if k:
            pltpu.make_async_remote_copy(
                src_ref=part.at[b], dst_ref=part_slots.at[k - 1], send_sem=b_send, recv_sem=b_recv,
                device_id=(my_dp, b), device_id_type=MESH,
            ).start()
    own, norms = sq[my_mp], norm_buf[...]
    drain(sq_slots, s_recv)
    drain(norm_slots, n_recv)
    for k in range(MP - 1):
        own = own + sq_slots[k]
        norms = norms + norm_slots[k]
    own = own[0:1] * own[1:2]
    bases = [own + norms[:, t:t + 1] * norms[:, STEPS + t:STEPS + t + 1] for t in range(STEPS)]
    total = part[my_mp]
    drain(part_slots, b_recv)
    for k in range(MP - 1):
        total = total + part_slots[k]
    row = jnp.zeros((1, LANES), f32)
    low = None
    for t in range(STEPS):
        cross = total[t:t + 1] * total[STEPS + t:STEPS + t + 1]
        dist = jnp.maximum(bases[t] - 2.0 * cross, 0.0)
        low = dist if low is None else jnp.minimum(low, dist)
        row = jnp.where(lane1 == t, jnp.sum(low, axis=1, keepdims=True), row)
    row_buf[...] = row
    for kd in reversed(range(DP)):
        for km in reversed(range(MP)):
            if kd or km:
                pltpu.make_async_remote_copy(
                    src_ref=row_buf, dst_ref=row_slots.at[pl.ds(me, 1)],
                    send_sem=d_send, recv_sem=d_recv,
                    device_id=(dp_peers[kd], mp_peers[km]), device_id_type=MESH,
                ).start()
    row_slots[pl.ds(me, 1), :] = row
    dist_ref[...] = low
    drain(ch_slots, a_send)
    drain(sq_slots, s_send)
    drain(norm_slots, n_send)
    drain(part_slots, b_send)
    others = row_slots.at[pl.ds(0, DP * MP - 1)]
    drain(others, d_send)
    drain(others, d_recv)
    mean_ref[...] = jnp.sum(row_slots[...], axis=0, keepdims=True) / (blk * MP * DP)


def solution(mesh):
    DP, MP = mesh.shape["dp"], mesh.shape["mp"]

    def body(hidden_states, factor_values, class_ids, centers):
        rows, width = hidden_states.shape
        depth = class_ids.shape[1]
        blk = rows // MP
        vm = pltpu.VMEM
        sem = pltpu.SemaphoreType.DMA
        hbm = pl.BlockSpec(memory_space=pl.ANY)
        low, mean = pl.pallas_call(
            functools.partial(kernel, DP, MP),
            out_shape=(vm((1, blk), jnp.float32), vm((1, LANES), jnp.float32)),
            in_specs=[hbm] * 4,
            out_specs=(pl.BlockSpec(memory_space=vm), pl.BlockSpec(memory_space=vm)),
            scratch_shapes=[
                pltpu.SMEM((STEPS,), jnp.int32),
                vm((rows // TALL, TALL, width), jnp.bfloat16),
                vm((rows // LANES, depth, LANES), jnp.bfloat16),
                vm((rows // LANES, depth, LANES), jnp.int32),
                vm((4, width), jnp.bfloat16),
                vm((DP - 1, 4, width), jnp.bfloat16),
                vm((MP, 2, blk), jnp.float32),
                vm((MP - 1, 2, blk), jnp.float32),
                vm((1, LANES), jnp.float32),
                vm((MP - 1, 1, LANES), jnp.float32),
                vm((MP, 2 * STEPS, blk), jnp.float32),
                vm((MP - 1, 2 * STEPS, blk), jnp.float32),
                vm((1, LANES), jnp.float32),
                vm((DP * MP, LANES), jnp.float32),
                *[sem] * 14,
            ],
            compiler_params=pltpu.CompilerParams(collective_id=0, has_side_effects=True),
        )(centers, hidden_states.reshape(rows // TALL, TALL, width), factor_values.T, class_ids.T)
        spec = pl.BlockSpec(memory_space=vm)
        return pl.pallas_call(
            finish,
            out_shape=(
                jax.ShapeDtypeStruct((blk,), jnp.float32),
                jax.ShapeDtypeStruct((STEPS,), jnp.float32),
            ),
            in_specs=[spec, spec],
            out_specs=(spec, spec),
        )(
            pltpu.with_memory_space_constraint(low.reshape(blk), vm),
            pltpu.with_memory_space_constraint(mean.reshape(LANES), vm),
        )

    return jax.shard_map(
        body,
        mesh=mesh,
        in_specs=(P("dp", "mp"), P("dp", "mp"), P("dp", "mp"), P()),
        out_specs=(P(("dp", "mp")), P()),
        check_vma=False,
    )
```

profile of v0, /device:TPU:1, one launch (start us, length us, event | category | flops | bytes accessed | tf_op | source)
XLA Modules:
  0.0 26.2 jit_solution(17512870056547391238)
XLA Ops:
  0.6 25.0 %shard_map.59 = (f32[1,512]{1,0:T(1,128)S(1)}, f32[1,128]{1,0:T(1,128)S(1)}) custom-call(s32[3]{0:T(128)} %c_hbm.1, bf16[256,16,512]{2,1,0:T(8,128)(2,1)} %bitcast.7, bf16[16,4096]{1,0:T(8,128)(2,1)} %bitcast.9, s32[16,4096]{1,0:T(8,128)} %bitcast.8), custom_call_target="tpu_custom_call" | custom-call | tf_op jit(solution)/shard_map/pallas_call | solution.py:237
  25.6 0.6 %shard_map.60 = (f32[512]{0:T(512)}, f32[3]{0:T(128)}) custom-call(f32[512]{0:T(512)S(1)} %bitcast.5, f32[128]{0:T(128)S(1)} %bitcast.6), custom_call_target="tpu_custom_call" | custom-call | tf_op jit(solution)/shard_map/pallas_call | solution.py:262
where the time goes:
time: 26.3 us; the launch traced here: 26.2 us
  Pallas kernels  25.5 us (97%)
  between operations  0.64 us (2%)
    pallas_call x1, Pallas kernels, body(): pl.pallas_call(functools.partial(kernel, DP, MP), out_shape=(vm((1, blk),...  25 us
    pallas_call x1, Pallas kernels, body(): pl.pallas_call(finish, out_shape=(jax.ShapeDtypeStruct((blk,), jnp.float3...  0.58 us

commit v1 on v0

v1 whole, which is shorter than its diff:
```python
import functools

import jax
import jax.numpy as jnp
from jax import lax
from jax.experimental import pallas as pl
from jax.experimental.pallas import tpu as pltpu
from jax.sharding import PartitionSpec as P

MESH = pl.DeviceIdType.MESH
STEPS = 3
LANES = 128
TALL = 16
CHUNKS = 8
VOCAB = 128256
NT = (((1,), (1,)), ((), ()))
NN = (((1,), (0,)), ((), ()))
DP_ORDER = (13, 12, 15, 11, 14, 10, 9, 5, 8, 4, 7, 3, 6, 2, 1)
MP_ORDER = (5, 4, 7, 3, 6, 2, 1)


def partner(p, k):
    bit = 1
    q = p
    while bit <= k:
        if k & bit:
            q = q + bit - 2 * bit * lax.rem(lax.div(p, bit), 2)
        bit *= 2
    return q


def drain(ref, sem):
    pltpu.make_async_copy(ref, ref, sem).wait()


def encode(k, base):
    local = k - base
    high = local >> 7
    x = (local & 127).astype(jnp.float32) * (1.0 / 128.0) + 1.0
    for j in range(7):
        x = jnp.where((high & (1 << j)) != 0, x * (2.0 ** (1 << j)), x)
    return x


def tiled(x):
    rows, depth = x.shape
    return x.T.reshape(depth // 8, 8, rows // LANES, LANES).transpose(0, 2, 1, 3)


def finish(low_ref, mean_ref, dist_ref, means_ref):
    dist_ref[...] = low_ref[...]
    means_ref[...] = mean_ref[0:STEPS]


def kernel(DP, MP, *refs):
    h = refs[7]
    width = h.shape[2]
    rows = h.shape[0] * h.shape[1]
    depth = refs[9].shape[0] * refs[9].shape[2]
    tiles = rows // LANES
    pl.run_scoped(
        functools.partial(steps, DP, MP, *refs),
        pltpu.VMEM((tiles, width, LANES), jnp.bfloat16),
        pltpu.VMEM((tiles, depth, LANES), jnp.bfloat16),
        pltpu.VMEM((STEPS * 2 * depth, depth, LANES), jnp.bfloat16),
    )


def steps(
    DP, MP,
    c_hbm, h_hbm, v_hbm, i_hbm,
    dist_ref, mean_ref,
    c_ref, h, v, ids, vals, ch_buf, ch_slots, sq, sq_slots, part, own_ref, part_slots,
    row_buf, row_slots,
    z_sem, h_sem, i_sem, v_sem, a_send, a_recv, s_send, s_recv, b_send, b_recv,
    d_send, d_recv, flip, code, splat,
):
    groups, tall, width = h.shape
    rows = groups * tall
    halves = ids.shape[0]
    depth = halves * ids.shape[2]
    blk = rows // MP
    my_dp = lax.axis_index("dp")
    my_mp = lax.axis_index("mp")
    me = my_dp * MP + my_mp
    f32, bf16 = jnp.float32, jnp.bfloat16
    dp_peers = [partner(my_dp, k) for k in range(DP)]
    mp_peers = [partner(my_mp, k) for k in range(MP)]

    step = max(groups // CHUNKS, 1)
    for j in range(0, groups, step):
        at = pl.ds(j, step)
        pltpu.make_async_copy(h_hbm.at[at], h.at[at], h_sem).start()
    pltpu.make_async_copy(c_hbm, c_ref, z_sem).start()
    pltpu.make_async_copy(i_hbm, ids, i_sem).start()
    pltpu.make_async_copy(v_hbm, v, v_sem).start()
    barrier = pltpu.get_barrier_semaphore()
    for k in DP_ORDER:
        pl.semaphore_signal(barrier, inc=1, device_id=(dp_peers[k], my_mp), device_id_type=MESH)
    for k in MP_ORDER:
        pl.semaphore_signal(barrier, inc=1, device_id=(my_dp, mp_peers[k]), device_id_type=MESH)

    pltpu.make_async_copy(c_hbm, c_ref, z_sem).wait()
    drain(ids, i_sem)
    drain(v, v_sem)

    base = my_mp * (VOCAB // MP)
    lane = lax.broadcasted_iota(jnp.int32, (2 * depth, LANES), 1)
    row16 = lax.broadcasted_iota(jnp.int32, (tall, 1), 0)
    ones = jnp.ones((8, LANES), bf16)
    first = my_dp * rows
    offs = [lax.rem(c_ref[t], rows) for t in range(STEPS)]
    found = []
    for t in range(STEPS):
        g = lax.div(offs[t], LANES)
        own = [ids[i, g] for i in range(halves)] + [v[i, g].astype(f32) for i in range(halves)]
        own[:halves] = [encode(x, base) for x in own[:halves]]
        both = jnp.concatenate(own, axis=0)
        hit = lane + (first + g * LANES) == c_ref[t]
        found.append(jnp.where(hit, both, 0.0))
    found.append(jnp.zeros((LANES - STEPS * 2 * depth, LANES), f32))
    meta = lax.dot_general(
        ones, jnp.concatenate(found, axis=0).astype(bf16), NT, preferred_element_type=f32
    )[0:1]
    meta = jnp.concatenate([meta, jnp.zeros((1, width - LANES), f32)], axis=1)
    drain(h, h_sem)
    picks = []
    for t in range(STEPS):
        g = lax.div(offs[t], tall)
        hit = row16 + (first + g * tall) == c_ref[t]
        picks.append(jnp.sum(jnp.where(hit, h[g].astype(f32), 0.0), axis=0, keepdims=True))
    picks.append(meta)
    ch_buf[...] = jnp.concatenate(picks, axis=0).astype(bf16)

    pl.semaphore_wait(barrier, DP - 1 + MP - 1)
    for k in DP_ORDER:
        pltpu.make_async_remote_copy(
            src_ref=ch_buf, dst_ref=ch_slots.at[k - 1], send_sem=a_send, recv_sem=a_recv,
            device_id=(dp_peers[k], my_mp), device_id_type=MESH,
        ).start()

    tiles = blk // LANES
    for b in range(MP):
        turned = h[b * blk // tall:(b + 1) * blk // tall].reshape(blk, width).T
        for j in range(tiles):
            x = turned[:, j * LANES:(j + 1) * LANES]
            flip[b * tiles + j] = x
            x = x.astype(f32)
            sq[b, 0:1, j * LANES:(j + 1) * LANES] = jnp.sum(x * x, axis=0, keepdims=True)
            at = b * tiles + j
            a = jnp.concatenate([v[i, at].astype(f32) for i in range(halves)], axis=0)
            vals[at] = a
            sq[b, 1:2, j * LANES:(j + 1) * LANES] = jnp.sum(a * a, axis=0, keepdims=True)
            k = jnp.concatenate([ids[i, at] for i in range(halves)], axis=0)
            code[at] = encode(k, base).astype(bf16)
    for k in MP_ORDER:
        pltpu.make_async_remote_copy(
            src_ref=sq.at[mp_peers[k]], dst_ref=sq_slots.at[k - 1], send_sem=s_send, recv_sem=s_recv,
            device_id=(my_dp, mp_peers[k]), device_id_type=MESH,
        ).start()

    drain(ch_slots, a_recv)
    ch4 = ch_buf[...]
    for d in range(DP - 1):
        ch4 = ch4 + ch_slots[d]
    ch4 = ch4.astype(f32)
    row8 = lax.broadcasted_iota(jnp.int32, (8, 1), 0)
    ch8 = jnp.concatenate([ch4, jnp.zeros_like(ch4)], axis=0)
    ch = jnp.where(row8 < STEPS, ch8, 0.0)
    meta = ch4[3:4, 0:LANES]
    nh = jnp.sum(ch * ch, axis=1, keepdims=True)
    lane1 = lax.broadcasted_iota(jnp.int32, (1, LANES), 1)
    ch = jnp.concatenate([ch, jnp.zeros_like(ch)], axis=0).astype(bf16)
    norms = jnp.zeros((1, LANES), f32)
    for t in range(STEPS):
        here = (lane1 >= (2 * t + 1) * depth) & (lane1 < (2 * t + 2) * depth)
        na = jnp.sum(jnp.where(here, meta * meta, 0.0), axis=1, keepdims=True)
        norms = jnp.where(lane1 == t, nh[t:t + 1], norms)
        norms = jnp.where(lane1 == STEPS + t, na, norms)
    norms = jnp.concatenate([norms, jnp.zeros((1, blk - LANES), f32)], axis=1)
    norms_hi = norms.astype(bf16).astype(f32)
    norms_lo = norms - norms_hi
    tail = jnp.where(row8 == 2 * STEPS, norms_hi, jnp.where(row8 == 2 * STEPS + 1, norms_lo, 0.0))
    cols = jnp.broadcast_to(meta, (LANES, LANES)).T
    for r in range(STEPS * 2 * depth):
        splat[r] = jnp.broadcast_to(cols[r:r + 1], (depth, LANES)).astype(bf16)

    for k in MP_ORDER + (0,):
        b = mp_peers[k]
        hb = jnp.concatenate([flip[b * tiles + j] for j in range(tiles)], axis=1)
        total = lax.dot_general(ch, hb, NN, preferred_element_type=f32)[0:8] + tail
        cb = [code[b * tiles + j] for j in range(tiles)]
        for t in range(STEPS):
            w = [jnp.zeros((depth, LANES), bf16) for _ in range(tiles)]
            for l in range(depth):
                kl = splat[2 * depth * t + l]
                vl = splat[2 * depth * t + depth + l]
                for j in range(tiles):
                    w[j] = jnp.where(cb[j] == kl, vl, w[j])
            aa = jnp.concatenate(
                [
                    jnp.sum(vals[b * tiles + j] * w[j].astype(f32), axis=0, keepdims=True)
                    for j in range(tiles)
                ],
                axis=1,
            )
            total = jnp.where(row8 == STEPS + t, aa, total)
        if k:
            part[b] = total.astype(bf16)
            pltpu.make_async_remote_copy(
                src_ref=part.at[b], dst_ref=part_slots.at[k - 1], send_sem=b_send, recv_sem=b_recv,
                device_id=(my_dp, b), device_id_type=MESH,
            ).start()
        else:
            own_ref[...] = total
    own = sq[my_mp]
    drain(sq_slots, s_recv)
    for k in range(MP - 1):
        own = own + sq_slots[k]
    own = own[0:1] * own[1:2]
    total = own_ref[...]
    drain(part_slots, b_recv)
    for k in range(MP - 1):
        total = total + part_slots[k].astype(f32)
    norms = total[2 * STEPS:2 * STEPS + 1] + total[2 * STEPS + 1:2 * STEPS + 2]
    row = jnp.zeros((1, LANES), f32)
    low = None
    for t in range(STEPS):
        cross = total[t:t + 1] * total[STEPS + t:STEPS + t + 1]
        far = own + norms[:, t:t + 1] * norms[:, STEPS + t:STEPS + t + 1]
        dist = jnp.maximum(far - 2.0 * cross, 0.0)
        low = dist if low is None else jnp.minimum(low, dist)
        row = jnp.where(lane1 == t, jnp.sum(low, axis=1, keepdims=True), row)
    row_buf[...] = row
    for kd in DP_ORDER + (0,):
        for km in MP_ORDER + (0,):
            if kd or km:
                pltpu.make_async_remote_copy(
                    src_ref=row_buf, dst_ref=row_slots.at[pl.ds(me, 1)],
                    send_sem=d_send, recv_sem=d_recv,
                    device_id=(dp_peers[kd], mp_peers[km]), device_id_type=MESH,
                ).start()
    row_slots[pl.ds(me, 1), :] = row
    dist_ref[...] = low
    drain(ch_slots, a_send)
    drain(sq_slots, s_send)
    drain(part_slots, b_send)
    others = row_slots.at[pl.ds(0, DP * MP - 1)]
    drain(others, d_send)
    drain(others, d_recv)
    mean_ref[...] = jnp.sum(row_slots[...], axis=0, keepdims=True) / (blk * MP * DP)


def solution(mesh):
    DP, MP = mesh.shape["dp"], mesh.shape["mp"]

    def body(hidden_states, factor_values, class_ids, centers):
        rows, width = hidden_states.shape
        depth = class_ids.shape[1]
        blk = rows // MP
        vm = pltpu.VMEM
        sem = pltpu.SemaphoreType.DMA
        hbm = pl.BlockSpec(memory_space=pl.ANY)
        low, mean = pl.pallas_call(
            functools.partial(kernel, DP, MP),
            out_shape=(vm((1, blk), jnp.float32), vm((1, LANES), jnp.float32)),
            in_specs=[hbm] * 4,
            out_specs=(pl.BlockSpec(memory_space=vm), pl.BlockSpec(memory_space=vm)),
            scratch_shapes=[
                pltpu.SMEM((STEPS,), jnp.int32),
                vm((rows // TALL, TALL, width), jnp.bfloat16),
                vm((depth // 8, rows // LANES, 8, LANES), jnp.bfloat16),
                vm((depth // 8, rows // LANES, 8, LANES), jnp.int32),
                vm((rows // LANES, depth, LANES), jnp.float32),
                vm((4, width), jnp.bfloat16),
                vm((DP - 1, 4, width), jnp.bfloat16),
                vm((MP, 2, blk), jnp.float32),
                vm((MP - 1, 2, blk), jnp.float32),
                vm((MP, 8, blk), jnp.bfloat16),
                vm((8, blk), jnp.float32),
                vm((MP - 1, 8, blk), jnp.bfloat16),
                vm((1, LANES), jnp.float32),
                vm((DP * MP, LANES), jnp.float32),
                *[sem] * 12,
            ],
            compiler_params=pltpu.CompilerParams(collective_id=0, has_side_effects=True),
        )(
            centers, hidden_states.reshape(rows // TALL, TALL, width),
            tiled(factor_values), tiled(class_ids),
        )
        spec = pl.BlockSpec(memory_space=vm)
        return pl.pallas_call(
            finish,
            out_shape=(
                jax.ShapeDtypeStruct((blk,), jnp.float32),
                jax.ShapeDtypeStruct((STEPS,), jnp.float32),
            ),
            in_specs=[spec, spec],
            out_specs=(spec, spec),
        )(
            pltpu.with_memory_space_constraint(low.reshape(blk), vm),
            pltpu.with_memory_space_constraint(mean.reshape(LANES), vm),
        )

    return jax.shard_map(
        body,
        mesh=mesh,
        in_specs=(P("dp", "mp"), P("dp", "mp"), P("dp", "mp"), P()),
        out_specs=(P(("dp", "mp")), P()),
        check_vma=False,
    )
```

time: 26.3 us -> 25.5 us (0.970)
  Pallas kernels: 25.5 us -> 24.7 us
    pallas_call x1, Pallas kernels: 25 us -> 24.1 us  [body(): pl.pallas_call(functools.partial(kernel, DP, MP), out_shape=(vm((1, blk),...]
where the time goes in v1:
time: 25.5 us; the launch traced here: 25.4 us
  Pallas kernels  24.7 us (97%)
  between operations  0.64 us (3%)
    pallas_call x1, Pallas kernels, body(): pl.pallas_call(functools.partial(kernel, DP, MP), out_shape=(vm((1, blk),...  24.1 us
    pallas_call x1, Pallas kernels, body(): pl.pallas_call(finish, out_shape=(jax.ShapeDtypeStruct((blk,), jnp.float3...  0.58 us

profile of v1, /device:TPU:1, one launch (start us, length us, event | category | flops | bytes accessed | tf_op | source)
XLA Modules:
  0.0 25.4 jit_solution(5173982136876484948)
XLA Ops:
  0.6 24.1 %shard_map.59 = (f32[1,512]{1,0:T(1,128)S(1)}, f32[1,128]{1,0:T(1,128)S(1)}) custom-call(s32[3]{0:T(128)} %refs_0_.1, bf16[256,16,512]{2,1,0:T(8,128)(2,1)} %bitcast.15, bf16[2,32,8,128]{3,2,1,0:T(8,128)(2,1)} %bitcast.17, s32[2,32,8,128]{3,2,1,0:T(8,128)} %bitcast.16), custom_call_target="tpu_custom_call" | custom-call | tf_op jit(solution)/shard_map/pallas_call | solution.py:264
  24.8 0.6 %shard_map.60 = (f32[512]{0:T(512)}, f32[3]{0:T(128)}) custom-call(f32[512]{0:T(512)S(1)} %bitcast.13, f32[128]{0:T(128)S(1)} %bitcast.14), custom_call_target="tpu_custom_call" | custom-call | tf_op jit(solution)/shard_map/pallas_call | solution.py:292
